TPU v7x, 256 devices: a whole 4x4x8 slice. The times are simulated.
256 devices in a mesh: section: 16 (over y, z_hi), tp: 16 (over x, z_lo, core).
Axes of the slice: x: 4, y: 4, z: 8 (z_hi: 4, z_lo: 2; z = z_hi * 2 + z_lo), core: 2. Of those that a mesh axis runs over, the one named last changes fastest.
Arguments:
- incoming: bfloat16 [16, 256, 6144], P('section', 'tp'), may hold values from -11 to 11, as said below
- grad_in: bfloat16 [16, 256, 6144], P('section', 'tp'), may hold values from -6 to 6
- held: bfloat16 [16, 2, 256, 6144], P('section', None, 'tp'), may hold values from -11 to 11, as said below
- roster: int32 [16, 2], replicated, may hold values from 0 to 1
- norm_gain: float32 [16, 6144], P('section'), may hold values from 0.25 to 1.75
- r_scores: float32 [16, 48, 256, 256], P('section', 'tp'), may hold values from -12 to 236
- value_weight: bfloat16 [16, 6144, 6144], P('section', None, 'tp'), may hold values from -0.078125 to 0.078125
- out_weight: bfloat16 [16, 6144, 6144], P('section', 'tp'), may hold values from -0.078125 to 0.078125
Outputs:
- act_out: bfloat16 [16, 256, 6144], P('section', 'tp')
- grad_out: bfloat16 [16, 256, 6144], P('section', 'tp')
- held_next: bfloat16 [16, 2, 256, 6144], P('section', None, 'tp')
Inputs may be any that keep to these rules, and one draw needn't show every extreme that they name: `incoming`: every token row has its own scale. `held`: every token row has its own scale. roster[s, 0] names the slot at section 15 - s that holds section s's stash to fetch; roster[s, 1] names the slot there that takes section s's evicted input; the two may be equal.
All inputs are finite; a program needn't handle non-finite values.
Results may differ from a plain program's by a relative error of at most 0.0036.
Values may be sent and summed in bfloat16 or wider, within the bound.
No kernel may reach another device: no remote copies, remote signals or barrier semaphores. Data moves between devices by JAX's collectives and lax.ppermute only.
A program may use at most 64 MiB of HBM per device.

v0:
```python
import functools

import jax
import jax.numpy as jnp
from jax import lax
from jax.experimental import pallas as pl
from jax.experimental.pallas import tpu as pltpu
from jax.sharding import PartitionSpec as P


EPS = 0.5

A, B, Z, CORE = 4, 12, 2, 1
PLACE = {A: 1, B: 2, Z: 4}
HALVES = ((A, B), (B, A))
ROWS = 32


def trade(value, distance):
    return lax.ppermute(value, "tp", [(i, i ^ distance) for i in range(16)])


def place(order, first, second):
    return first * PLACE[order[0]] + second * PLACE[order[1]]


def row_scale(values):
    return jnp.sqrt(jnp.mean(values * values, axis=-1, keepdims=True) + EPS)


def call(kernel, outs, args, scratch=(), smem=0, mib=6):
    vmem = pl.BlockSpec(memory_space=pltpu.VMEM)
    in_specs = [pl.BlockSpec(memory_space=pltpu.SMEM)] * smem + [vmem] * (len(args) - smem)
    return pl.pallas_call(
        kernel,
        out_shape=outs,
        in_specs=in_specs,
        out_specs=[vmem] * len(outs),
        scratch_shapes=list(scratch),
        compiler_params=pltpu.CompilerParams(vmem_limit_bytes=mib * 1024 * 1024),
    )(*args)


def core_here():
    return lax.axis_index("tp") & 1


def dot(left, right, left_dim, right_dim):
    return lax.dot_general(
        left, right, (((left_dim,), (right_dim,)), ((), ())), preferred_element_type=jnp.float32
    )


def columns(start, size):
    return pl.ds(pl.multiple_of(start, 128), size)


def fill(z_first, pieces, rows):
    part = rows.shape[1] // 2
    for t, order in enumerate(HALVES):
        for late in range(2):
            for mid in range(2):
                for early in range(2):
                    first, z = (mid, early) if z_first else (early, mid)
                    to = (place(order, first, late) + z * PLACE[Z]) * ROWS
                    at = (mid * 2 + early) * ROWS
                    rows[to : to + ROWS, t * part : (t + 1) * part] = pieces[2 * t + late][at : at + ROWS, :]


def first_b_kernel(*refs):
    pieces, own, other, out, rows = refs[:4], refs[4], refs[5], refs[6], refs[7]
    fill(True, pieces, rows)
    half, heads = rows.shape[1], own.shape[0]
    out[:, :heads] = dot(rows[...], own[:, columns(core_here() * half, half)], 1, 1)
    out[:, heads:] = dot(rows[...], other[...], 1, 1)


def first_f_kernel(*refs):
    pieces, own, other, out, rows = refs[:4], refs[4], refs[5], refs[6], refs[7]
    fill(False, pieces, rows)
    half, heads = rows.shape[1], own.shape[1]
    out[:, :heads] = dot(rows[...], own[columns(core_here() * half, half), :], 1, 0)
    out[:, heads:] = dot(rows[...], other[...], 1, 0)


def mix(probs_dim, mine, theirs, probs, probs_other, mixed):
    width = mine.shape[1] // 2
    head = 128
    for half, chances in enumerate((probs, probs_other)):
        for h in range(width // head):
            at = half * width + h * head
            across = (1 - half) * width + h * head
            whole = (mine[:, at : at + head] + theirs[:, across : across + head]).astype(jnp.bfloat16)
            mixed[:, at : at + head] = dot(chances[h], whole, probs_dim, 0).astype(jnp.bfloat16)


STEP = 256


def second_kernel(bwd, mine, theirs, probs, probs_other, own, other, *refs):
    outs, mixed = refs[:4], refs[4]
    mix(0 if bwd else 1, mine, theirs, probs, probs_other, mixed)
    heads, part = other.shape[1 if bwd else 0], outs[0].shape[1]
    start = core_here() * (2 * part)
    for t, order in enumerate(HALVES):
        send, keep = outs[2 * t], outs[2 * t + 1]
        for c in range(0, part, STEP):
            at = t * part + c
            if bwd:
                total = dot(mixed[:, :heads], own[columns(start + at, STEP), :], 1, 1)
                total = total + dot(mixed[:, heads:], other[at : at + STEP, :], 1, 1)
            else:
                total = dot(mixed[:, :heads], own[:, columns(start + at, STEP)], 1, 0)
                total = total + dot(mixed[:, heads:], other[:, at : at + STEP], 1, 0)
            for mid in range(2):
                for late in range(2):
                    z, second = (mid, late) if bwd else (late, mid)
                    to = (mid * 2 + late) * ROWS
                    row = (place(order, 0, second) + z * PLACE[Z]) * ROWS
                    keep[to : to + ROWS, c : c + STEP] = total[row : row + ROWS]
                    row = (place(order, 1, second) + z * PLACE[Z]) * ROWS
                    send[to : to + ROWS, c : c + STEP] = total[row : row + ROWS].astype(jnp.bfloat16)


def add_z_kernel(kept, came, *outs):
    part = outs[0].shape[1]
    for t in range(2):
        cols = slice(t * part, (t + 1) * part)
        total = kept[:, cols] + came[:, cols].astype(jnp.float32)
        outs[2 * t][...] = total[ROWS:].astype(jnp.bfloat16)
        outs[2 * t + 1][...] = total[:ROWS]


def add_kernel(*refs):
    ins, outs = refs[:4], refs[4:]
    for t in range(2):
        kept, came = ins[2 * t], ins[2 * t + 1]
        rows = kept.shape[0] // 2
        if len(outs) == 2:
            send = outs[0].at[:, t * kept.shape[1] : (t + 1) * kept.shape[1]]
            keep = outs[1].at[:, t * kept.shape[1] : (t + 1) * kept.shape[1]]
        else:
            send, keep = outs[2 * t], outs[2 * t + 1]
        keep[...] = kept[:rows] + came[:rows].astype(jnp.float32)
        send[...] = (kept[rows:] + came[rows:].astype(jnp.float32)).astype(jnp.bfloat16)


def last_add_b_kernel(*refs):
    ins, go, stay = refs[:4], refs[4], refs[5]
    rows = ROWS // 2
    core = core_here()
    for t in range(2):
        kept, came = ins[2 * t], ins[2 * t + 1]
        part = kept.shape[1]
        for out, which in ((go, 1 - core), (stay, core)):
            at = pl.multiple_of(which * rows, rows)
            sums = kept[pl.ds(at, rows), :] + came[pl.ds(at, rows), :].astype(jnp.float32)
            out[:, t * part : (t + 1) * part] = sums


def last_add_f_kernel(kept, came, go, stay):
    rows = ROWS // 2
    core = core_here()
    for out, which in ((go, 1 - core), (stay, core)):
        at = pl.multiple_of(which * rows, rows)
        out[...] = kept[pl.ds(at, rows), :] + came[pl.ds(at, rows), :].astype(jnp.float32)


def split_kernel(rows, go, stay):
    half = go.shape[1]
    lower = core_here() == 0
    go[...] = jnp.where(lower, rows[:, half:], rows[:, :half])
    stay[...] = jnp.where(lower, rows[:, :half], rows[:, half:])


def norm_kernel(rows, gain, go, stay):
    half = go.shape[1]
    values = rows[...].astype(jnp.float32)
    normed = (values / row_scale(values) * gain[...]).astype(jnp.bfloat16)
    lower = core_here() == 0
    go[...] = jnp.where(lower, normed[:, half:], normed[:, :half])
    stay[...] = jnp.where(lower, normed[:, :half], normed[:, half:])


def block_kernel(stay, came, *outs):
    rows, part = stay.shape[0], outs[0].shape[1]
    lower = core_here() == 0
    for t, out in enumerate(outs):
        mine, other = stay[:, t * part : (t + 1) * part], came[:, t * part : (t + 1) * part]
        out[:rows] = jnp.where(lower, mine, other)
        out[rows:] = jnp.where(lower, other, mine)


def split_join_kernel(had, came, *outs):
    rows, part = had.shape[0], outs[0].shape[1]
    for t, out in enumerate(outs):
        out[:rows] = had[:, t * part : (t + 1) * part]
        out[rows:] = came[:, t * part : (t + 1) * part]


def join_kernel(*refs):
    ins, outs = refs[:4], refs[4:]
    for t in range(2):
        had, came = ins[2 * t], ins[2 * t + 1]
        rows, part = had.shape
        out = outs[t] if len(outs) == 2 else outs[0].at[:, t * part : (t + 1) * part]
        out[:rows] = had[...]
        out[rows:] = came[...]


def copy_kernel(value, out):
    out[...] = value[...]


def whole(stay, came):
    lower = core_here() == 0
    return jnp.concatenate(
        [jnp.where(lower, stay[...], came[...]), jnp.where(lower, came[...], stay[...])], axis=1
    )


def end_f_kernel(stay, came, tokens, out):
    out[...] = (tokens[...].astype(jnp.float32) + whole(stay, came)).astype(jnp.bfloat16)


def end_b_kernel(stay, came, grads, stash, gain, out):
    weighted = gain[...] * whole(stay, came)
    stash_f32 = stash[...].astype(jnp.float32)
    scale = row_scale(stash_f32)
    inner_sum = jnp.sum(weighted * stash_f32, axis=-1, keepdims=True)
    width = stash_f32.shape[1]
    out[...] = (
        grads[...].astype(jnp.float32) + weighted / scale - stash_f32 * inner_sum / (width * (scale * scale * scale))
    ).astype(jnp.bfloat16)


def give_out_kernel(weights, out):
    half = out.shape[1]
    out[...] = weights[:, columns((1 - core_here()) * half, half)]


def give_value_kernel(weights, out):
    half = out.shape[0]
    out[...] = weights[columns((1 - core_here()) * half, half), :]


def probs_kernel(scores, out):
    length = scores.shape[1]
    row = lax.broadcasted_iota(jnp.int32, (length, length), 0)
    col = lax.broadcasted_iota(jnp.int32, (length, length), 1)
    tp = lax.axis_index("tp")
    at = row >> 5
    token = (((tp >> 2) ^ (at & 1) ^ (((at >> 1) & 1) * 3)) << 6) | ((((tp >> 1) & 1) ^ (at >> 2)) << 5) | (row & 31)
    order = (token == col).astype(jnp.bfloat16)
    allowed = col <= row
    for h in range(scores.shape[0]):
        masked = jnp.where(allowed, scores[h], -jnp.inf)
        highest = jnp.max(masked, axis=-1, keepdims=True)
        expo = jnp.exp(masked - highest)
        probs = (expo / jnp.sum(expo, axis=-1, keepdims=True)).astype(jnp.bfloat16)
        probs = dot(order, probs, 1, 0).astype(jnp.bfloat16)
        out[h] = dot(probs, order, 1, 1).astype(jnp.bfloat16)


def stash_kernel(roster, store, out):
    out[...] = store[roster[0, 15 - lax.axis_index("section")]]


def held_kernel(roster, store, came, out):
    slot = roster[1, 15 - lax.axis_index("section")]
    for i in range(store.shape[0]):
        out[i] = jnp.where(slot == i, came[...], store[i])


def part_trades(distances, values):
    return [trade(value, distance) for value, distance in zip(values, distances)]


def body(incoming, grad_in, held, roster, norm_gain, r_scores, value_weight, out_weight):
    tokens_here = incoming[0]
    grad_here = grad_in[0]
    stash_store = held[0]
    gain = norm_gain[0]
    w_value = value_weight[0]
    w_out = out_weight[0]
    width = tokens_here.shape[1]
    half = width // 2
    part = half // 2
    bf16, f32 = jnp.bfloat16, jnp.float32
    sections = lax.axis_size("section")
    ring = range(sections)
    shape = jax.ShapeDtypeStruct

    halved = [shape((ROWS // 2, half), bf16)] * 2

    def pieces(rows, came):
        return [piece for pair in zip(rows, came) for piece in pair]

    def blocks(go, stay, count):
        came = trade(go, CORE)
        return call(block_kernel, [shape((ROWS, half // count), bf16)] * count, [stay, came])

    def wide(rows):
        return [shape((rows, part), bf16)] * 2

    grads = blocks(*call(split_kernel, halved, [grad_here]), 1)[0]
    grads = call(split_join_kernel, wide(2 * ROWS), [grads, trade(grads, Z)])
    grads = call(join_kernel, wide(4 * ROWS), pieces(grads, part_trades((A, B), grads)))
    grads_came = part_trades((B, A), grads)
    normed = blocks(*call(norm_kernel, halved, [tokens_here, gain[None]]), 2)
    joined = [shape((2 * ROWS, half), bf16)]
    normed = call(join_kernel, joined, pieces(normed, part_trades((A, B), normed)))[0]
    normed = call(split_join_kernel, wide(4 * ROWS), [normed, trade(normed, Z)])
    normed_came = part_trades((B, A), normed)

    heads_width = w_out.shape[0]
    out_give = call(give_out_kernel, [shape((heads_width, half), bf16)], [w_out], mib=9)[0]
    out_other = trade(out_give, CORE)
    value_give = call(give_value_kernel, [shape((half, heads_width), bf16)], [w_value], mib=9)[0]
    value_other = trade(value_give, CORE)

    seq_len = r_scores.shape[2]
    probs = call(probs_kernel, [shape(r_scores.shape[1:], bf16)], [r_scores[0]])[0]
    probs_other = trade(probs, CORE)

    outgoing = call(stash_kernel, [shape(tokens_here.shape, bf16)], [roster.T, stash_store], smem=1)[0]
    mirrored = [(s, sections - 1 - s) for s in ring]
    arriving = lax.ppermute(tokens_here, "section", mirrored)
    fetched = lax.ppermute(outgoing, "section", mirrored)
    held_next = call(held_kernel, [shape(stash_store.shape, bf16)], [roster.T, stash_store, arriving], smem=1)[0]

    partial = [shape((seq_len, 2 * heads_width), f32)]
    rows_scratch = [pltpu.VMEM((seq_len, half), bf16)]
    mixed_scratch = [pltpu.VMEM((seq_len, 2 * heads_width), bf16)]

    def sums(rows, width):
        return [shape((rows, width), t) for t in (bf16, f32)]

    args = pieces(grads, grads_came) + [w_out, out_other]
    mine_b = call(first_b_kernel, partial, args, rows_scratch, mib=16)[0]
    args = [mine_b, trade(mine_b, CORE), probs, probs_other, w_value, value_other]
    kernel = functools.partial(second_kernel, True)
    parts_b = call(kernel, sums(4 * ROWS, part) * 2, args, mixed_scratch, mib=20)
    args = pieces(normed, normed_came) + [w_value, value_other]
    mine_f = call(first_f_kernel, partial, args, rows_scratch, mib=16)[0]
    args = [mine_f, trade(mine_f, CORE), probs, probs_other, w_out, out_other]
    kernel = functools.partial(second_kernel, False)
    parts_f = call(kernel, sums(4 * ROWS, part) * 2, args, mixed_scratch, mib=20)

    last = [shape((ROWS // 2, half), f32)] * 2
    ended = [shape(tokens_here.shape, bf16)]
    came = part_trades((A, B), parts_b[0::2])
    send, keep = call(add_kernel, sums(2 * ROWS, half), pieces(parts_b[1::2], came))
    parts = call(add_z_kernel, sums(ROWS, part) * 2, [keep, trade(send, Z)])
    came = part_trades((B, A), parts[0::2])
    go, stay = call(last_add_b_kernel, last, pieces(parts[1::2], came))
    args = [stay, trade(go, CORE), grad_here, fetched, gain[None]]
    input_grad = call(end_b_kernel, ended, args)[0]

    came = part_trades((A, B), parts_f[0::2])
    parts = call(add_kernel, sums(2 * ROWS, part) * 2, pieces(parts_f[1::2], came))
    came = part_trades((B, A), parts[0::2])
    send, keep = call(add_kernel, sums(ROWS, half), pieces(parts[1::2], came))
    go, stay = call(last_add_f_kernel, last, [keep, trade(send, Z)])
    args = [stay, trade(go, CORE), tokens_here]
    layer_out = call(end_f_kernel, ended, args)[0]
    returned = lax.ppermute(input_grad, "section", [(s, (s - 1) % sections) for s in ring])
    passed_on = lax.ppermute(layer_out, "section", [(s, (s + 1) % sections) for s in ring])
    returned = call(copy_kernel, ended, [returned])[0]
    passed_on = call(copy_kernel, ended, [passed_on])[0]
    return (passed_on[None], returned[None], held_next[None])


def solution(mesh):
    in_specs = (
        P("section", "tp", None),
        P("section", "tp", None),
        P("section", None, "tp", None),
        P(),
        P("section", None),
        P("section", "tp", None, None),
        P("section", None, "tp"),
        P("section", "tp", None),
    )
    out_specs = (P("section", "tp", None), P("section", "tp", None), P("section", None, "tp", None))

    return jax.shard_map(body, mesh=mesh, in_specs=in_specs, out_specs=out_specs, check_vma=False)
```

profile of v0, /device:TPU:4, one launch (start us, length us, event | category | flops | bytes accessed | tf_op | source)
XLA Modules:
  0.0 124.5 jit_solution(15769555248607286603)
XLA Ops:
  0.6 2.3 %copy-done.1 = bf16[1,384,6144]{2,1,0:T(8,128)(2,1)S(1)} copy-done((bf16[1,384,6144]{2,1,0:T(8,128)(2,1)S(1)}, bf16[1,384,6144]{2,1,0:T(8,128)(2,1)}, u32[]{:S(2)}) %copy-start.1) | copy-done | bytes 4718616
  3.2 2.1 %copy-done = bf16[1,6144,384]{2,1,0:T(8,128)(2,1)S(1)} copy-done((bf16[1,6144,384]{2,1,0:T(8,128)(2,1)S(1)}, bf16[1,6144,384]{2,1,0:T(8,128)(2,1)}, u32[]{:S(2)}) %copy-start) | copy-done | bytes 4718616
  6.6 4.6 %collective-permute-done.17.came = bf16[16,3072]{1,0:T(8,128)(2,1)S(1)} collective-permute-done((bf16[16,3072]{1,0:T(8,128)(2,1)S(1)}, bf16[16,3072]{1,0:T(8,128)(2,1)S(1)}, u32[]{:S(2)}, u32[]{:S(2)}) %collective-permute-start.17) | collective-permute-done | bytes 98336 | tf_op jit(solution)/shard_map/ppermute | solution.py:20
  11.3 2.0 %collective-permute-start.18 = (bf16[32,3072]{1,0:T(8,128)(2,1)S(1)}, bf16[32,3072]{1,0:T(8,128)(2,1)S(1)}, u32[]{:S(2)}, u32[]{:S(2)}) collective-permute-start(bf16[32,3072]{1,0:T(8,128)(2,1)S(1)} %shard_map.118.had), channel_id=1, source_target_pairs={{0,2},{1,3},{2,0},{3,1},{4,6},{5,7},{6,4},{7,5},{8,10},{9,11},{10,... | collective-permute-start | bytes 589832 | tf_op jit(solution)/shard_map/ppermute | solution.py:20
  16.2 2.3 %collective-permute-done.18.came = bf16[32,3072]{1,0:T(8,128)(2,1)S(1)} collective-permute-done((bf16[32,3072]{1,0:T(8,128)(2,1)S(1)}, bf16[32,3072]{1,0:T(8,128)(2,1)S(1)}, u32[]{:S(2)}, u32[]{:S(2)}) %collective-permute-start.18) | collective-permute-done | bytes 196640 | tf_op jit(solution)/shard_map/ppermute | solution.py:20
  21.8 6.1 %collective-permute-done.2.refs_3_ = bf16[32,1536]{1,0:T(8,128)(2,1)S(1)} collective-permute-done((bf16[32,1536]{1,0:T(8,128)(2,1)S(1)}, bf16[32,1536]{1,0:T(8,128)(2,1)S(1)}, u32[]{:S(2)}, u32[]{:S(2)}) %collective-permute-start.2) | collective-permute-done | bytes 98336 | tf_op jit(solution)/shard_map/ppermute | solution.py:20
  30.0 2.9 %collective-permute-start.22 = (bf16[128,1536]{1,0:T(8,128)(2,1)S(1)}, bf16[128,1536]{1,0:T(8,128)(2,1)S(1)}, u32[]{:S(2)}, u32[]{:S(2)}) collective-permute-start(bf16[128,1536]{1,0:T(8,128)(2,1)S(1)} %get-tuple-element.62.refs_2_), channel_id=1, source_target_pairs={{0,4},{1,5},{2,6},{3,7},{4,0},{5,1},{6,2},{7,3},{8,12},{9,13},{10,... | collective-permute-start | bytes 1179656 | tf_op jit(solution)/shard_map/ppermute | solution.py:20
  32.9 4.4 %collective-permute-done.3.came = bf16[64,3072]{1,0:T(8,128)(2,1)S(1)} collective-permute-done((bf16[64,3072]{1,0:T(8,128)(2,1)S(1)}, bf16[64,3072]{1,0:T(8,128)(2,1)S(1)}, u32[]{:S(2)}, u32[]{:S(2)}) %collective-permute-start.3) | collective-permute-done | bytes 393248 | tf_op jit(solution)/shard_map/ppermute | solution.py:20
  39.7 3.2 %collective-permute-start.5 = (bf16[128,1536]{1,0:T(8,128)(2,1)S(1)}, bf16[128,1536]{1,0:T(8,128)(2,1)S(1)}, u32[]{:S(2)}, u32[]{:S(2)}) collective-permute-start(bf16[128,1536]{1,0:T(8,128)(2,1)S(1)} %get-tuple-element.44.refs_2_), channel_id=1, source_target_pairs={{0,4},{1,5},{2,6},{3,7},{4,0},{5,1},{6,2},{7,3},{8,12},{9,13},{10,... | collective-permute-start | bytes 1179656 | tf_op jit(solution)/shard_map/ppermute | solution.py:20
  43.0 1.8 %shard_map.121.mine = f32[256,768]{1,0:T(8,128)S(1)} custom-call(bf16[128,1536]{1,0:T(8,128)(2,1)S(1)} %get-tuple-element.61.refs_0_, bf16[128,1536]{1,0:T(8,128)(2,1)S(1)} %collective-permute-done.21.refs_1_, bf16[128,1536]{1,0:T(8,128)(2,1)S(1)} %get-tuple-element.62.refs_2_, bf16[128,1536]{1,0:T(8,128)(2,1)S(1)} %collective-permute-done.22.refs_3_, ...), custom_call_target="tpu_custom_call" | custom-call | tf_op jit(solution)/shard_map/pallas_call | solution.py:34
  45.1 2.0 %collective-permute-done.4.refs_1_ = bf16[128,1536]{1,0:T(8,128)(2,1)S(1)} collective-permute-done((bf16[128,1536]{1,0:T(8,128)(2,1)S(1)}, bf16[128,1536]{1,0:T(8,128)(2,1)S(1)}, u32[]{:S(2)}, u32[]{:S(2)}) %collective-permute-start.4) | collective-permute-done | bytes 393248 | tf_op jit(solution)/shard_map/ppermute | solution.py:20
  48.7 1.8 %shard_map.108.mine = f32[256,768]{1,0:T(8,128)S(1)} custom-call(bf16[128,1536]{1,0:T(8,128)(2,1)S(1)} %get-tuple-element.43.refs_0_, bf16[128,1536]{1,0:T(8,128)(2,1)S(1)} %collective-permute-done.4.refs_1_, bf16[128,1536]{1,0:T(8,128)(2,1)S(1)} %get-tuple-element.44.refs_2_, bf16[128,1536]{1,0:T(8,128)(2,1)S(1)} %collective-permute-done.5.refs_3_, ...), custom_call_target="tpu_custom_call" | custom-call | tf_op jit(solution)/shard_map/pallas_call | solution.py:34
  53.4 2.1 %shard_map.122 = (bf16[128,1536]{1,0:T(8,128)(2,1)S(1)}, f32[128,1536]{1,0:T(8,128)S(1)}, bf16[128,1536]{1,0:T(8,128)(2,1)S(1)}, f32[128,1536]{1,0:T(8,128)S(1)}) custom-call(f32[256,768]{1,0:T(8,128)S(1)} %shard_map.121.mine, f32[256,768]{1,0:T(8,128)S(1)} %collective-permute-done.23.theirs, bf16[3,256,256]{2,1,0:T(8,128)(2,1)S(1)} %shard_map.109.probs, ...), custom_call_target="tpu_custom_call" | custom-call | tf_op jit(solution)/shard_map/pallas_call | solution.py:34
  55.6 2.1 %collective-permute-start.24 = (bf16[128,1536]{1,0:T(8,128)(2,1)S(1)}, bf16[128,1536]{1,0:T(8,128)(2,1)S(1)}, u32[]{:S(2)}, u32[]{:S(2)}) collective-permute-start(bf16[128,1536]{1,0:T(8,128)(2,1)S(1)} %get-tuple-element.64), channel_id=1, source_target_pairs={{0,4},{1,5},{2,6},{3,7},{4,0},{5,1},{6,2},{7,3},{8,12},{9,13},{10,... | collective-permute-start | bytes 1179656 | tf_op jit(solution)/shard_map/ppermute | solution.py:20
  58.4 2.1 %shard_map.111 = (bf16[128,1536]{1,0:T(8,128)(2,1)S(1)}, f32[128,1536]{1,0:T(8,128)S(1)}, bf16[128,1536]{1,0:T(8,128)(2,1)S(1)}, f32[128,1536]{1,0:T(8,128)S(1)}) custom-call(f32[256,768]{1,0:T(8,128)S(1)} %shard_map.108.mine, f32[256,768]{1,0:T(8,128)S(1)} %collective-permute-done.7.theirs, bf16[3,256,256]{2,1,0:T(8,128)(2,1)S(1)} %shard_map.109.probs, ...), custom_call_target="tpu_custom_call" | custom-call | tf_op jit(solution)/shard_map/pallas_call | solution.py:34
  62.6 5.0 %collective-permute-done.24.refs_1_ = bf16[128,1536]{1,0:T(8,128)(2,1)S(1)} collective-permute-done((bf16[128,1536]{1,0:T(8,128)(2,1)S(1)}, bf16[128,1536]{1,0:T(8,128)(2,1)S(1)}, u32[]{:S(2)}, u32[]{:S(2)}) %collective-permute-start.24) | collective-permute-done | bytes 393248 | tf_op jit(solution)/shard_map/ppermute | solution.py:20
  67.6 2.0 %collective-permute-done.25.refs_3_ = bf16[128,1536]{1,0:T(8,128)(2,1)S(1)} collective-permute-done((bf16[128,1536]{1,0:T(8,128)(2,1)S(1)}, bf16[128,1536]{1,0:T(8,128)(2,1)S(1)}, u32[]{:S(2)}, u32[]{:S(2)}) %collective-permute-start.25) | collective-permute-done | bytes 393248 | tf_op jit(solution)/shard_map/ppermute | solution.py:20
  70.1 5.5 %collective-permute-done.10.refs_1_ = bf16[128,1536]{1,0:T(8,128)(2,1)S(1)} collective-permute-done((bf16[128,1536]{1,0:T(8,128)(2,1)S(1)}, bf16[128,1536]{1,0:T(8,128)(2,1)S(1)}, u32[]{:S(2)}, u32[]{:S(2)}) %collective-permute-start.10) | collective-permute-done | bytes 393248 | tf_op jit(solution)/shard_map/ppermute | solution.py:20
  78.1 2.2 %collective-permute-start.13 = (bf16[64,1536]{1,0:T(8,128)(2,1)S(1)}, bf16[64,1536]{1,0:T(8,128)(2,1)S(1)}, u32[]{:S(2)}, u32[]{:S(2)}) collective-permute-start(bf16[64,1536]{1,0:T(8,128)(2,1)S(1)} %get-tuple-element.52), channel_id=1, source_target_pairs={{0,4},{1,5},{2,6},{3,7},{4,0},{5,1},{6,2},{7,3},{8,12},{9,13},{10,... | collective-permute-start | bytes 589832 | tf_op jit(solution)/shard_map/ppermute | solution.py:20
  80.3 3.0 %collective-permute-done.12.refs_1_ = bf16[64,1536]{1,0:T(8,128)(2,1)S(1)} collective-permute-done((bf16[64,1536]{1,0:T(8,128)(2,1)S(1)}, bf16[64,1536]{1,0:T(8,128)(2,1)S(1)}, u32[]{:S(2)}, u32[]{:S(2)}) %collective-permute-start.12) | collective-permute-done | bytes 196640 | tf_op jit(solution)/shard_map/ppermute | solution.py:20
  86.1 2.3 %collective-permute-start.28 = (bf16[32,1536]{1,0:T(8,128)(2,1)S(1)}, bf16[32,1536]{1,0:T(8,128)(2,1)S(1)}, u32[]{:S(2)}, u32[]{:S(2)}) collective-permute-start(bf16[32,1536]{1,0:T(8,128)(2,1)S(1)} %get-tuple-element.72), channel_id=1, source_target_pairs={{0,4},{1,5},{2,6},{3,7},{4,0},{5,1},{6,2},{7,3},{8,12},{9,13},{10,... | collective-permute-start | bytes 294920 | tf_op jit(solution)/shard_map/ppermute | solution.py:20
  89.1 8.7 %collective-permute-start.30 = (bf16[16,6144]{1,0:T(8,128)(2,1)S(1)}, bf16[16,6144]{1,0:T(8,128)(2,1)S(1)}, u32[]{:S(2)}, u32[]{:S(2)}) collective-permute-start(bf16[16,6144]{1,0:T(8,128)(2,1)S(1)} %shard_map.126), channel_id=1, source_target_pairs={{0,240},{16,224},{32,208},{48,192},{64,176},{80,160},{96,144},{112... | collective-permute-start | bytes 589832 | tf_op jit(solution)/shard_map/ppermute | solution.py:329
  101.5 9.9 %collective-permute-done.30.stash = bf16[16,6144]{1,0:T(8,128)(2,1)S(1)} collective-permute-done((bf16[16,6144]{1,0:T(8,128)(2,1)S(1)}, bf16[16,6144]{1,0:T(8,128)(2,1)S(1)}, u32[]{:S(2)}, u32[]{:S(2)}) %collective-permute-start.30) | collective-permute-done | bytes 196640 | tf_op jit(solution)/shard_map/ppermute | solution.py:329
  111.7 8.9 %collective-permute-start.31 = (bf16[16,6144]{1,0:T(8,128)(2,1)S(1)}, bf16[16,6144]{1,0:T(8,128)(2,1)S(1)}, u32[]{:S(2)}, u32[]{:S(2)}) collective-permute-start(bf16[16,6144]{1,0:T(8,128)(2,1)S(1)} %shard_map.127), channel_id=1, source_target_pairs={{0,240},{16,0},{32,16},{48,32},{64,48},{80,64},{96,80},{112,96},{1... | collective-permute-start | bytes 589832 | tf_op jit(solution)/shard_map/ppermute | solution.py:367
  (90 shorter events, 34.0 us)
Async XLA Ops:
  3.1 39.8 %collective-permute-start.9 = (bf16[384,3072]{1,0:T(8,128)(2,1)S(1)}, bf16[384,3072]{1,0:T(8,128)(2,1)S(1)}, u32[]{:S(2)}, u32[]{:S(2)}) collective-permute-start(bf16[384,3072]{1,0:T(8,128)(2,1)S(1)} %shard_map.110), channel_id=1, source_target_pairs={{0,1},{1,0},{2,3},{3,2},{4,5},{5,4},{6,7},{7,6},{8,9},{9,8},{10,11... | collective-permute-start | bytes 7077896 | tf_op jit(solution)/shard_map/ppermute | solution.py:20
  5.5 43.1 %collective-permute-start.6 = (bf16[3072,384]{1,0:T(8,128)(2,1)S(1)}, bf16[3072,384]{1,0:T(8,128)(2,1)S(1)}, u32[]{:S(2)}, u32[]{:S(2)}) collective-permute-start(bf16[3072,384]{1,0:T(8,128)(2,1)S(1)} %shard_map.107), channel_id=1, source_target_pairs={{0,1},{1,0},{2,3},{3,2},{4,5},{5,4},{6,7},{7,6},{8,9},{9,8},{10,11... | collective-permute-start | bytes 7077896 | tf_op jit(solution)/shard_map/ppermute | solution.py:20
  18.5 11.1 %collective-permute-start.19 = (bf16[64,1536]{1,0:T(8,128)(2,1)S(1)}, bf16[64,1536]{1,0:T(8,128)(2,1)S(1)}, u32[]{:S(2)}, u32[]{:S(2)}) collective-permute-start(bf16[64,1536]{1,0:T(8,128)(2,1)S(1)} %get-tuple-element.59.refs_0_), channel_id=1, source_target_pairs={{0,4},{1,5},{2,6},{3,7},{4,0},{5,1},{6,2},{7,3},{8,12},{9,13},{10,... | collective-permute-start | bytes 589832 | tf_op jit(solution)/shard_map/ppermute | solution.py:20
  19.8 9.8 %collective-permute-start.20 = (bf16[64,1536]{1,0:T(8,128)(2,1)S(1)}, bf16[64,1536]{1,0:T(8,128)(2,1)S(1)}, u32[]{:S(2)}, u32[]{:S(2)}) collective-permute-start(bf16[64,1536]{1,0:T(8,128)(2,1)S(1)} %get-tuple-element.60.refs_2_), channel_id=1, source_target_pairs={{0,12},{1,13},{2,14},{3,15},{4,8},{5,9},{6,10},{7,11},{8,4},{9,5},... | collective-permute-start | bytes 589832 | tf_op jit(solution)/shard_map/ppermute | solution.py:20
  27.9 9.4 %collective-permute-start.3 = (bf16[64,3072]{1,0:T(8,128)(2,1)S(1)}, bf16[64,3072]{1,0:T(8,128)(2,1)S(1)}, u32[]{:S(2)}, u32[]{:S(2)}) collective-permute-start(bf16[64,3072]{1,0:T(8,128)(2,1)S(1)} %shard_map.105.had), channel_id=1, source_target_pairs={{0,2},{1,3},{2,0},{3,1},{4,6},{5,7},{6,4},{7,5},{8,10},{9,11},{10,... | collective-permute-start | bytes 1179656 | tf_op jit(solution)/shard_map/ppermute | solution.py:20
  29.6 10.0 %collective-permute-start.21 = (bf16[128,1536]{1,0:T(8,128)(2,1)S(1)}, bf16[128,1536]{1,0:T(8,128)(2,1)S(1)}, u32[]{:S(2)}, u32[]{:S(2)}) collective-permute-start(bf16[128,1536]{1,0:T(8,128)(2,1)S(1)} %get-tuple-element.61.refs_0_), channel_id=1, source_target_pairs={{0,12},{1,13},{2,14},{3,15},{4,8},{5,9},{6,10},{7,11},{8,4},{9,5},... | collective-permute-start | bytes 1179656 | tf_op jit(solution)/shard_map/ppermute | solution.py:20
  30.0 12.9 %collective-permute-start.22 = (bf16[128,1536]{1,0:T(8,128)(2,1)S(1)}, bf16[128,1536]{1,0:T(8,128)(2,1)S(1)}, u32[]{:S(2)}, u32[]{:S(2)}) collective-permute-start(bf16[128,1536]{1,0:T(8,128)(2,1)S(1)} %get-tuple-element.62.refs_2_), channel_id=1, source_target_pairs={{0,4},{1,5},{2,6},{3,7},{4,0},{5,1},{6,2},{7,3},{8,12},{9,13},{10,... | collective-permute-start | bytes 1179656 | tf_op jit(solution)/shard_map/ppermute | solution.py:20
  37.4 9.6 %collective-permute-start.4 = (bf16[128,1536]{1,0:T(8,128)(2,1)S(1)}, bf16[128,1536]{1,0:T(8,128)(2,1)S(1)}, u32[]{:S(2)}, u32[]{:S(2)}) collective-permute-start(bf16[128,1536]{1,0:T(8,128)(2,1)S(1)} %get-tuple-element.43.refs_0_), channel_id=1, source_target_pairs={{0,12},{1,13},{2,14},{3,15},{4,8},{5,9},{6,10},{7,11},{8,4},{9,5},... | collective-permute-start | bytes 1179656 | tf_op jit(solution)/shard_map/ppermute | solution.py:20
  39.7 9.0 %collective-permute-start.5 = (bf16[128,1536]{1,0:T(8,128)(2,1)S(1)}, bf16[128,1536]{1,0:T(8,128)(2,1)S(1)}, u32[]{:S(2)}, u32[]{:S(2)}) collective-permute-start(bf16[128,1536]{1,0:T(8,128)(2,1)S(1)} %get-tuple-element.44.refs_2_), channel_id=1, source_target_pairs={{0,4},{1,5},{2,6},{3,7},{4,0},{5,1},{6,2},{7,3},{8,12},{9,13},{10,... | collective-permute-start | bytes 1179656 | tf_op jit(solution)/shard_map/ppermute | solution.py:20
  44.8 8.7 %collective-permute-start.23 = (f32[256,768]{1,0:T(8,128)S(1)}, f32[256,768]{1,0:T(8,128)S(1)}, u32[]{:S(2)}, u32[]{:S(2)}) collective-permute-start(f32[256,768]{1,0:T(8,128)S(1)} %shard_map.121.mine), channel_id=1, source_target_pairs={{0,1},{1,0},{2,3},{3,2},{4,5},{5,4},{6,7},{7,6},{8,9},{9,8},{10,11... | collective-permute-start | bytes 2359304 | tf_op jit(solution)/shard_map/ppermute | solution.py:20
  50.5 7.9 %collective-permute-start.7 = (f32[256,768]{1,0:T(8,128)S(1)}, f32[256,768]{1,0:T(8,128)S(1)}, u32[]{:S(2)}, u32[]{:S(2)}) collective-permute-start(f32[256,768]{1,0:T(8,128)S(1)} %shard_map.108.mine), channel_id=1, source_target_pairs={{0,1},{1,0},{2,3},{3,2},{4,5},{5,4},{6,7},{7,6},{8,9},{9,8},{10,11... | collective-permute-start | bytes 2359304 | tf_op jit(solution)/shard_map/ppermute | solution.py:20
  55.6 12.1 %collective-permute-start.24 = (bf16[128,1536]{1,0:T(8,128)(2,1)S(1)}, bf16[128,1536]{1,0:T(8,128)(2,1)S(1)}, u32[]{:S(2)}, u32[]{:S(2)}) collective-permute-start(bf16[128,1536]{1,0:T(8,128)(2,1)S(1)} %get-tuple-element.64), channel_id=1, source_target_pairs={{0,4},{1,5},{2,6},{3,7},{4,0},{5,1},{6,2},{7,3},{8,12},{9,13},{10,... | collective-permute-start | bytes 1179656 | tf_op jit(solution)/shard_map/ppermute | solution.py:20
  57.7 12.0 %collective-permute-start.25 = (bf16[128,1536]{1,0:T(8,128)(2,1)S(1)}, bf16[128,1536]{1,0:T(8,128)(2,1)S(1)}, u32[]{:S(2)}, u32[]{:S(2)}) collective-permute-start(bf16[128,1536]{1,0:T(8,128)(2,1)S(1)} %get-tuple-element.66), channel_id=1, source_target_pairs={{0,12},{1,13},{2,14},{3,15},{4,8},{5,9},{6,10},{7,11},{8,4},{9,5},... | collective-permute-start | bytes 1179656 | tf_op jit(solution)/shard_map/ppermute | solution.py:20
  60.5 15.1 %collective-permute-start.10 = (bf16[128,1536]{1,0:T(8,128)(2,1)S(1)}, bf16[128,1536]{1,0:T(8,128)(2,1)S(1)}, u32[]{:S(2)}, u32[]{:S(2)}) collective-permute-start(bf16[128,1536]{1,0:T(8,128)(2,1)S(1)} %get-tuple-element.46), channel_id=1, source_target_pairs={{0,4},{1,5},{2,6},{3,7},{4,0},{5,1},{6,2},{7,3},{8,12},{9,13},{10,... | collective-permute-start | bytes 1179656 | tf_op jit(solution)/shard_map/ppermute | solution.py:20
  61.5 15.6 %collective-permute-start.11 = (bf16[128,1536]{1,0:T(8,128)(2,1)S(1)}, bf16[128,1536]{1,0:T(8,128)(2,1)S(1)}, u32[]{:S(2)}, u32[]{:S(2)}) collective-permute-start(bf16[128,1536]{1,0:T(8,128)(2,1)S(1)} %get-tuple-element.48), channel_id=1, source_target_pairs={{0,12},{1,13},{2,14},{3,15},{4,8},{5,9},{6,10},{7,11},{8,4},{9,5},... | collective-permute-start | bytes 1179656 | tf_op jit(solution)/shard_map/ppermute | solution.py:20
  69.8 15.3 %collective-permute-start.26 = (bf16[64,3072]{1,0:T(8,128)(2,1)S(1)}, bf16[64,3072]{1,0:T(8,128)(2,1)S(1)}, u32[]{:S(2)}, u32[]{:S(2)}) collective-permute-start(bf16[64,3072]{1,0:T(8,128)(2,1)S(1)} %get-tuple-element.68), channel_id=1, source_target_pairs={{0,2},{1,3},{2,0},{3,1},{4,6},{5,7},{6,4},{7,5},{8,10},{9,11},{10,... | collective-permute-start | bytes 1179656 | tf_op jit(solution)/shard_map/ppermute | solution.py:20
  84.3 13.4 %collective-permute-start.14 = (bf16[32,3072]{1,0:T(8,128)(2,1)S(1)}, bf16[32,3072]{1,0:T(8,128)(2,1)S(1)}, u32[]{:S(2)}, u32[]{:S(2)}) collective-permute-start(bf16[32,3072]{1,0:T(8,128)(2,1)S(1)} %get-tuple-element.54), channel_id=1, source_target_pairs={{0,2},{1,3},{2,0},{3,1},{4,6},{5,7},{6,4},{7,5},{8,10},{9,11},{10,... | collective-permute-start | bytes 589832 | tf_op jit(solution)/shard_map/ppermute | solution.py:20
  85.1 12.7 %collective-permute-start.27 = (bf16[32,1536]{1,0:T(8,128)(2,1)S(1)}, bf16[32,1536]{1,0:T(8,128)(2,1)S(1)}, u32[]{:S(2)}, u32[]{:S(2)}) collective-permute-start(bf16[32,1536]{1,0:T(8,128)(2,1)S(1)} %get-tuple-element.70), channel_id=1, source_target_pairs={{0,12},{1,13},{2,14},{3,15},{4,8},{5,9},{6,10},{7,11},{8,4},{9,5},... | collective-permute-start | bytes 294920 | tf_op jit(solution)/shard_map/ppermute | solution.py:20
  86.1 11.8 %collective-permute-start.28 = (bf16[32,1536]{1,0:T(8,128)(2,1)S(1)}, bf16[32,1536]{1,0:T(8,128)(2,1)S(1)}, u32[]{:S(2)}, u32[]{:S(2)}) collective-permute-start(bf16[32,1536]{1,0:T(8,128)(2,1)S(1)} %get-tuple-element.72), channel_id=1, source_target_pairs={{0,4},{1,5},{2,6},{3,7},{4,0},{5,1},{6,2},{7,3},{8,12},{9,13},{10,... | collective-permute-start | bytes 294920 | tf_op jit(solution)/shard_map/ppermute | solution.py:20
  89.1 22.3 %collective-permute-start.30 = (bf16[16,6144]{1,0:T(8,128)(2,1)S(1)}, bf16[16,6144]{1,0:T(8,128)(2,1)S(1)}, u32[]{:S(2)}, u32[]{:S(2)}) collective-permute-start(bf16[16,6144]{1,0:T(8,128)(2,1)S(1)} %shard_map.126), channel_id=1, source_target_pairs={{0,240},{16,224},{32,208},{48,192},{64,176},{80,160},{96,144},{112... | collective-permute-start | bytes 589832 | tf_op jit(solution)/shard_map/ppermute | solution.py:329
  97.9 13.5 %collective-permute-start.29 = (f32[16,3072]{1,0:T(8,128)S(1)}, f32[16,3072]{1,0:T(8,128)S(1)}, u32[]{:S(2)}, u32[]{:S(2)}) collective-permute-start(f32[16,3072]{1,0:T(8,128)S(1)} %get-tuple-element.74), channel_id=1, source_target_pairs={{0,1},{1,0},{2,3},{3,2},{4,5},{5,4},{6,7},{7,6},{8,9},{9,8},{10,11... | collective-permute-start | bytes 589832 | tf_op jit(solution)/shard_map/ppermute | solution.py:20
  98.5 22.1 %collective-permute-start.32 = (bf16[16,6144]{1,0:T(8,128)(2,1)S(1)}, bf16[16,6144]{1,0:T(8,128)(2,1)S(1)}, u32[]{:S(2)}, u32[]{:S(2)}) collective-permute-start(bf16[16,6144]{1,0:T(8,128)(2,1)S(1)} %bitcast.22), channel_id=1, source_target_pairs={{0,240},{16,224},{32,208},{48,192},{64,176},{80,160},{96,144},{112... | collective-permute-start | bytes 589832 | tf_op jit(solution)/shard_map/ppermute | solution.py:328
  99.9 22.0 %collective-permute-start.16 = (bf16[16,6144]{1,0:T(8,128)(2,1)S(1)}, bf16[16,6144]{1,0:T(8,128)(2,1)S(1)}, u32[]{:S(2)}, u32[]{:S(2)}) collective-permute-start(bf16[16,6144]{1,0:T(8,128)(2,1)S(1)} %shard_map.115), channel_id=1, source_target_pairs={{0,16},{16,32},{32,48},{48,64},{64,80},{80,96},{96,112},{112,128},... | collective-permute-start | bytes 589832 | tf_op jit(solution)/shard_map/ppermute | solution.py:368
  111.7 12.1 %collective-permute-start.31 = (bf16[16,6144]{1,0:T(8,128)(2,1)S(1)}, bf16[16,6144]{1,0:T(8,128)(2,1)S(1)}, u32[]{:S(2)}, u32[]{:S(2)}) collective-permute-start(bf16[16,6144]{1,0:T(8,128)(2,1)S(1)} %shard_map.127), channel_id=1, source_target_pairs={{0,240},{16,0},{32,16},{48,32},{64,48},{80,64},{96,80},{112,96},{1... | collective-permute-start | bytes 589832 | tf_op jit(solution)/shard_map/ppermute | solution.py:367
  (19 other events, 170.4 us)
where the time goes:
time: 125 us; the launch traced here: 124 us
  waiting for transfers between devices  54.1 us (43%)
  starting transfers between devices  50.7 us (41%)
  Pallas kernels  13.5 us (11%)
  local copies, waits for them, and re-layouts  5.3 us (4%)
    ppermute x29, waiting for transfers between devices, trade(): return lax.ppermute(value, 'tp', [(i, i ^ distance) for i in range(16)])  43 us
    ppermute x29, starting transfers between devices, trade(): return lax.ppermute(value, 'tp', [(i, i ^ distance) for i in range(16)])  30.2 us
    pallas_call x27, Pallas kernels, call(): pl.pallas_call(kernel, out_shape=outs, in_specs=in_specs, out_specs=[vmem...  13.5 us
    ppermute x1, waiting for transfers between devices, body(): fetched = lax.ppermute(outgoing, 'section', mirrored)  9.93 us
    ppermute x1, starting transfers between devices, body(): lax.ppermute(input_grad, 'section', [(s, (s - 1) % sections) for s in ring])  8.93 us
    ppermute x1, starting transfers between devices, body(): fetched = lax.ppermute(outgoing, 'section', mirrored)  8.67 us
    unnamed x20, local copies, waits for them, and re-layouts  5.3 us
  transfers between devices with their start and end apart: 33, of which 17 were waited for; matrix products, arithmetic and copies ran while one was open for 0% of the time, Pallas kernels for 10%

commit v1 on v0

--- a/solution.py
+++ b/solution.py
@@ -158,12 +158,17 @@
             out[:, t * part : (t + 1) * part] = sums
 
 
-def last_add_f_kernel(kept, came, go, stay):
+def add_f_kernel(*refs):
+    ins, same, cross, go, stay = refs[:4], refs[4], refs[5], refs[6], refs[7]
     rows = ROWS // 2
     core = core_here()
-    for out, which in ((go, 1 - core), (stay, core)):
-        at = pl.multiple_of(which * rows, rows)
-        out[...] = kept[pl.ds(at, rows), :] + came[pl.ds(at, rows), :].astype(jnp.float32)
+    for t in range(2):
+        kept, came = ins[2 * t], ins[2 * t + 1]
+        part = kept.shape[1]
+        for out, first, which in ((stay, 0, core), (go, 0, 1 - core), (same, ROWS, core), (cross, ROWS, 1 - core)):
+            at = pl.multiple_of(first + which * rows, rows)
+            sums = kept[pl.ds(at, rows), :] + came[pl.ds(at, rows), :].astype(jnp.float32)
+            out[:, t * part : (t + 1) * part] = sums.astype(out.dtype)
 
 
 def split_kernel(rows, go, stay):
@@ -219,8 +224,12 @@
     )
 
 
-def end_f_kernel(stay, came, tokens, out):
-    out[...] = (tokens[...].astype(jnp.float32) + whole(stay, came)).astype(jnp.bfloat16)
+def end_f_kernel(stay, same, kept, cross, tokens, out):
+    own = stay[...] + same[...].astype(jnp.float32)
+    other = kept[...] + cross[...].astype(jnp.float32)
+    lower = core_here() == 0
+    sums = jnp.concatenate([jnp.where(lower, own, other), jnp.where(lower, other, own)], axis=1)
+    out[...] = (tokens[...].astype(jnp.float32) + sums).astype(jnp.bfloat16)
 
 
 def end_b_kernel(stay, came, grads, stash, gain, out):
@@ -360,9 +369,9 @@
     came = part_trades((A, B), parts_f[0::2])
     parts = call(add_kernel, sums(2 * ROWS, part) * 2, pieces(parts_f[1::2], came))
     came = part_trades((B, A), parts[0::2])
-    send, keep = call(add_kernel, sums(ROWS, half), pieces(parts[1::2], came))
-    go, stay = call(last_add_f_kernel, last, [keep, trade(send, Z)])
-    args = [stay, trade(go, CORE), tokens_here]
+    ends = [shape((ROWS // 2, half), t) for t in (bf16, bf16, f32, f32)]
+    same, cross, go, stay = call(add_f_kernel, ends, pieces(parts[1::2], came))
+    args = [stay, trade(same, Z), trade(go, CORE), trade(cross, Z | CORE), tokens_here]
     layer_out = call(end_f_kernel, ended, args)[0]
     returned = lax.ppermute(input_grad, "section", [(s, (s - 1) % sections) for s in ring])
     passed_on = lax.ppermute(layer_out, "section", [(s, (s + 1) % sections) for s in ring])

time: 125 us -> 123 us (0.984)
  the two profiles are of different devices: /device:TPU:4 before, /device:TPU:33 now
where the time goes in v1:
time: 123 us
  waiting for transfers between devices  53.6 us (44%)
  starting transfers between devices  51.1 us (42%)
  Pallas kernels  13.5 us (11%)
  local copies, waits for them, and re-layouts  3.99 us (3%)
    ppermute x30, waiting for transfers between devices, trade(): return lax.ppermute(value, 'tp', [(i, i ^ distance) for i in range(16)])  41.1 us
    ppermute x30, starting transfers between devices, trade(): return lax.ppermute(value, 'tp', [(i, i ^ distance) for i in range(16)])  34.4 us
    pallas_call x26, Pallas kernels, call(): pl.pallas_call(kernel, out_shape=outs, in_specs=in_specs, out_specs=[vmem...  13.5 us
    ppermute x1, starting transfers between devices, body(): fetched = lax.ppermute(outgoing, 'section', mirrored)  8.24 us
    ppermute x1, waiting for transfers between devices, body(): lax.ppermute(layer_out, 'section', [(s, (s + 1) % sections) for s in ring])  6.84 us
    ppermute x1, waiting for transfers between devices, body(): arriving = lax.ppermute(tokens_here, 'section', mirrored)  5.66 us
    unnamed x20, local copies, waits for them, and re-layouts  3.99 us
    ppermute x1, starting transfers between devices, body(): lax.ppermute(input_grad, 'section', [(s, (s - 1) % sections) for s in ring])  3.16 us
  transfers between devices with their start and end apart: 34, of which 15 were waited for; matrix products, arithmetic and copies ran while one was open for 0% of the time, Pallas kernels for 10%

profile of v1, /device:TPU:33, one launch (start us, length us, event | category | flops | bytes accessed | tf_op | source)
XLA Modules:
  0.0 123.0 jit_solution(6640375446225854543)
XLA Ops:
  0.6 2.3 %copy-done.1 = bf16[1,384,6144]{2,1,0:T(8,128)(2,1)S(1)} copy-done((bf16[1,384,6144]{2,1,0:T(8,128)(2,1)S(1)}, bf16[1,384,6144]{2,1,0:T(8,128)(2,1)}, u32[]{:S(2)}) %copy-start.1) | copy-done | bytes 4718616
  7.3 4.3 %collective-permute-done.18.came = bf16[16,3072]{1,0:T(8,128)(2,1)S(1)} collective-permute-done((bf16[16,3072]{1,0:T(8,128)(2,1)S(1)}, bf16[16,3072]{1,0:T(8,128)(2,1)S(1)}, u32[]{:S(2)}, u32[]{:S(2)}) %collective-permute-start.18) | collective-permute-done | bytes 98336 | tf_op jit(solution)/shard_map/ppermute | solution.py:20
  15.3 2.7 %collective-permute-done.19.came = bf16[32,3072]{1,0:T(8,128)(2,1)S(1)} collective-permute-done((bf16[32,3072]{1,0:T(8,128)(2,1)S(1)}, bf16[32,3072]{1,0:T(8,128)(2,1)S(1)}, u32[]{:S(2)}, u32[]{:S(2)}) %collective-permute-start.19) | collective-permute-done | bytes 196640 | tf_op jit(solution)/shard_map/ppermute | solution.py:20
  19.1 1.8 %collective-permute-start.21 = (bf16[64,1536]{1,0:T(8,128)(2,1)S(1)}, bf16[64,1536]{1,0:T(8,128)(2,1)S(1)}, u32[]{:S(2)}, u32[]{:S(2)}) collective-permute-start(bf16[64,1536]{1,0:T(8,128)(2,1)S(1)} %get-tuple-element.60.refs_2_), channel_id=1, source_target_pairs={{0,12},{1,13},{2,14},{3,15},{4,8},{5,9},{6,10},{7,11},{8,4},{9,5},... | collective-permute-start | bytes 589832 | tf_op jit(solution)/shard_map/ppermute | solution.py:20
  21.8 5.6 %collective-permute-done.2.refs_3_ = bf16[32,1536]{1,0:T(8,128)(2,1)S(1)} collective-permute-done((bf16[32,1536]{1,0:T(8,128)(2,1)S(1)}, bf16[32,1536]{1,0:T(8,128)(2,1)S(1)}, u32[]{:S(2)}, u32[]{:S(2)}) %collective-permute-start.2) | collective-permute-done | bytes 98336 | tf_op jit(solution)/shard_map/ppermute | solution.py:20
  29.8 6.0 %collective-permute-done.3.came = bf16[64,3072]{1,0:T(8,128)(2,1)S(1)} collective-permute-done((bf16[64,3072]{1,0:T(8,128)(2,1)S(1)}, bf16[64,3072]{1,0:T(8,128)(2,1)S(1)}, u32[]{:S(2)}, u32[]{:S(2)}) %collective-permute-start.3) | collective-permute-done | bytes 393248 | tf_op jit(solution)/shard_map/ppermute | solution.py:20
  35.9 1.9 %collective-permute-start.4 = (bf16[128,1536]{1,0:T(8,128)(2,1)S(1)}, bf16[128,1536]{1,0:T(8,128)(2,1)S(1)}, u32[]{:S(2)}, u32[]{:S(2)}) collective-permute-start(bf16[128,1536]{1,0:T(8,128)(2,1)S(1)} %get-tuple-element.43.refs_0_), channel_id=1, source_target_pairs={{0,12},{1,13},{2,14},{3,15},{4,8},{5,9},{6,10},{7,11},{8,4},{9,5},... | collective-permute-start | bytes 1179656 | tf_op jit(solution)/shard_map/ppermute | solution.py:20
  37.9 1.8 %shard_map.120.mine = f32[256,768]{1,0:T(8,128)S(1)} custom-call(bf16[128,1536]{1,0:T(8,128)(2,1)S(1)} %get-tuple-element.61.refs_0_, bf16[128,1536]{1,0:T(8,128)(2,1)S(1)} %collective-permute-done.22.refs_1_, bf16[128,1536]{1,0:T(8,128)(2,1)S(1)} %get-tuple-element.62.refs_2_, bf16[128,1536]{1,0:T(8,128)(2,1)S(1)} %collective-permute-done.23.refs_3_, ...), custom_call_target="tpu_custom_call" | custom-call | tf_op jit(solution)/shard_map/pallas_call | solution.py:34
  39.7 4.3 %collective-permute-start.24 = (f32[256,768]{1,0:T(8,128)S(1)}, f32[256,768]{1,0:T(8,128)S(1)}, u32[]{:S(2)}, u32[]{:S(2)}) collective-permute-start(f32[256,768]{1,0:T(8,128)S(1)} %shard_map.120.mine), channel_id=1, source_target_pairs={{0,1},{1,0},{2,3},{3,2},{4,5},{5,4},{6,7},{7,6},{8,9},{9,8},{10,11... | collective-permute-start | bytes 2359304 | tf_op jit(solution)/shard_map/ppermute | solution.py:20
  44.0 2.2 %collective-permute-done.4.refs_1_ = bf16[128,1536]{1,0:T(8,128)(2,1)S(1)} collective-permute-done((bf16[128,1536]{1,0:T(8,128)(2,1)S(1)}, bf16[128,1536]{1,0:T(8,128)(2,1)S(1)}, u32[]{:S(2)}, u32[]{:S(2)}) %collective-permute-start.4) | collective-permute-done | bytes 393248 | tf_op jit(solution)/shard_map/ppermute | solution.py:20
  46.3 1.8 %shard_map.108.mine = f32[256,768]{1,0:T(8,128)S(1)} custom-call(bf16[128,1536]{1,0:T(8,128)(2,1)S(1)} %get-tuple-element.43.refs_0_, bf16[128,1536]{1,0:T(8,128)(2,1)S(1)} %collective-permute-done.4.refs_1_, bf16[128,1536]{1,0:T(8,128)(2,1)S(1)} %get-tuple-element.44.refs_2_, bf16[128,1536]{1,0:T(8,128)(2,1)S(1)} %collective-permute-done.5.refs_3_, ...), custom_call_target="tpu_custom_call" | custom-call | tf_op jit(solution)/shard_map/pallas_call | solution.py:34
  48.1 3.6 %collective-permute-start.7 = (f32[256,768]{1,0:T(8,128)S(1)}, f32[256,768]{1,0:T(8,128)S(1)}, u32[]{:S(2)}, u32[]{:S(2)}) collective-permute-start(f32[256,768]{1,0:T(8,128)S(1)} %shard_map.108.mine), channel_id=1, source_target_pairs={{0,1},{1,0},{2,3},{3,2},{4,5},{5,4},{6,7},{7,6},{8,9},{9,8},{10,11... | collective-permute-start | bytes 2359304 | tf_op jit(solution)/shard_map/ppermute | solution.py:20
  54.3 2.1 %shard_map.121 = (bf16[128,1536]{1,0:T(8,128)(2,1)S(1)}, f32[128,1536]{1,0:T(8,128)S(1)}, bf16[128,1536]{1,0:T(8,128)(2,1)S(1)}, f32[128,1536]{1,0:T(8,128)S(1)}) custom-call(f32[256,768]{1,0:T(8,128)S(1)} %shard_map.120.mine, f32[256,768]{1,0:T(8,128)S(1)} %collective-permute-done.24.theirs, bf16[3,256,256]{2,1,0:T(8,128)(2,1)S(1)} %shard_map.109.probs, ...), custom_call_target="tpu_custom_call" | custom-call | tf_op jit(solution)/shard_map/pallas_call | solution.py:34
  57.8 2.1 %shard_map.111 = (bf16[128,1536]{1,0:T(8,128)(2,1)S(1)}, f32[128,1536]{1,0:T(8,128)S(1)}, bf16[128,1536]{1,0:T(8,128)(2,1)S(1)}, f32[128,1536]{1,0:T(8,128)S(1)}) custom-call(f32[256,768]{1,0:T(8,128)S(1)} %shard_map.108.mine, f32[256,768]{1,0:T(8,128)S(1)} %collective-permute-done.7.theirs, bf16[3,256,256]{2,1,0:T(8,128)(2,1)S(1)} %shard_map.109.probs, ...), custom_call_target="tpu_custom_call" | custom-call | tf_op jit(solution)/shard_map/pallas_call | solution.py:34
  62.2 4.7 %collective-permute-done.25.refs_1_ = bf16[128,1536]{1,0:T(8,128)(2,1)S(1)} collective-permute-done((bf16[128,1536]{1,0:T(8,128)(2,1)S(1)}, bf16[128,1536]{1,0:T(8,128)(2,1)S(1)}, u32[]{:S(2)}, u32[]{:S(2)}) %collective-permute-start.25) | collective-permute-done | bytes 393248 | tf_op jit(solution)/shard_map/ppermute | solution.py:20
  69.4 6.0 %collective-permute-done.10.refs_1_ = bf16[128,1536]{1,0:T(8,128)(2,1)S(1)} collective-permute-done((bf16[128,1536]{1,0:T(8,128)(2,1)S(1)}, bf16[128,1536]{1,0:T(8,128)(2,1)S(1)}, u32[]{:S(2)}, u32[]{:S(2)}) %collective-permute-start.10) | collective-permute-done | bytes 393248 | tf_op jit(solution)/shard_map/ppermute | solution.py:20
  81.0 8.2 %collective-permute-start.31 = (bf16[16,6144]{1,0:T(8,128)(2,1)S(1)}, bf16[16,6144]{1,0:T(8,128)(2,1)S(1)}, u32[]{:S(2)}, u32[]{:S(2)}) collective-permute-start(bf16[16,6144]{1,0:T(8,128)(2,1)S(1)} %shard_map.125), channel_id=1, source_target_pairs={{0,240},{16,224},{32,208},{48,192},{64,176},{80,160},{96,144},{112... | collective-permute-start | bytes 589832 | tf_op jit(solution)/shard_map/ppermute | solution.py:338
  89.3 2.8 %collective-permute-start.15 = (f32[16,3072]{1,0:T(8,128)S(1)}, f32[16,3072]{1,0:T(8,128)S(1)}, u32[]{:S(2)}, u32[]{:S(2)}) collective-permute-start(f32[16,3072]{1,0:T(8,128)S(1)} %get-tuple-element.55), channel_id=1, source_target_pairs={{0,1},{1,0},{2,3},{3,2},{4,5},{5,4},{6,7},{7,6},{8,9},{9,8},{10,11... | collective-permute-start | bytes 589832 | tf_op jit(solution)/shard_map/ppermute | solution.py:20
  94.3 4.6 %collective-permute-done.14.same = bf16[16,3072]{1,0:T(8,128)(2,1)S(1)} collective-permute-done((bf16[16,3072]{1,0:T(8,128)(2,1)S(1)}, bf16[16,3072]{1,0:T(8,128)(2,1)S(1)}, u32[]{:S(2)}, u32[]{:S(2)}) %collective-permute-start.14) | collective-permute-done | bytes 98336 | tf_op jit(solution)/shard_map/ppermute | solution.py:20
  99.0 2.6 %collective-permute-start.33 = (bf16[16,6144]{1,0:T(8,128)(2,1)S(1)}, bf16[16,6144]{1,0:T(8,128)(2,1)S(1)}, u32[]{:S(2)}, u32[]{:S(2)}) collective-permute-start(bf16[16,6144]{1,0:T(8,128)(2,1)S(1)} %bitcast.24), channel_id=1, source_target_pairs={{0,240},{16,224},{32,208},{48,192},{64,176},{80,160},{96,144},{112... | collective-permute-start | bytes 589832 | tf_op jit(solution)/shard_map/ppermute | solution.py:337
  101.7 2.7 %collective-permute-start.17 = (bf16[16,6144]{1,0:T(8,128)(2,1)S(1)}, bf16[16,6144]{1,0:T(8,128)(2,1)S(1)}, u32[]{:S(2)}, u32[]{:S(2)}) collective-permute-start(bf16[16,6144]{1,0:T(8,128)(2,1)S(1)} %shard_map.114), channel_id=1, source_target_pairs={{0,16},{16,32},{32,48},{48,64},{64,80},{80,96},{96,112},{112,128},... | collective-permute-start | bytes 589832 | tf_op jit(solution)/shard_map/ppermute | solution.py:377
  104.7 3.2 %collective-permute-start.32 = (bf16[16,6144]{1,0:T(8,128)(2,1)S(1)}, bf16[16,6144]{1,0:T(8,128)(2,1)S(1)}, u32[]{:S(2)}, u32[]{:S(2)}) collective-permute-start(bf16[16,6144]{1,0:T(8,128)(2,1)S(1)} %shard_map.126), channel_id=1, source_target_pairs={{0,240},{16,0},{32,16},{48,32},{64,48},{80,64},{96,80},{112,96},{1... | collective-permute-start | bytes 589832 | tf_op jit(solution)/shard_map/ppermute | solution.py:376
  107.8 5.7 %collective-permute-done.33.came = bf16[16,6144]{1,0:T(8,128)(2,1)S(1)} collective-permute-done((bf16[16,6144]{1,0:T(8,128)(2,1)S(1)}, bf16[16,6144]{1,0:T(8,128)(2,1)S(1)}, u32[]{:S(2)}, u32[]{:S(2)}) %collective-permute-start.33) | collective-permute-done | bytes 196640 | tf_op jit(solution)/shard_map/ppermute | solution.py:337
  114.8 6.8 %collective-permute-done.17.value = bf16[16,6144]{1,0:T(8,128)(2,1)S(1)} collective-permute-done((bf16[16,6144]{1,0:T(8,128)(2,1)S(1)}, bf16[16,6144]{1,0:T(8,128)(2,1)S(1)}, u32[]{:S(2)}, u32[]{:S(2)}) %collective-permute-start.17) | collective-permute-done | bytes 196640 | tf_op jit(solution)/shard_map/ppermute | solution.py:377
  (91 shorter events, 32.4 us)
Async XLA Ops:
  3.1 34.7 %collective-permute-start.9 = (bf16[384,3072]{1,0:T(8,128)(2,1)S(1)}, bf16[384,3072]{1,0:T(8,128)(2,1)S(1)}, u32[]{:S(2)}, u32[]{:S(2)}) collective-permute-start(bf16[384,3072]{1,0:T(8,128)(2,1)S(1)} %shard_map.110), channel_id=1, source_target_pairs={{0,1},{1,0},{2,3},{3,2},{4,5},{5,4},{6,7},{7,6},{8,9},{9,8},{10,11... | collective-permute-start | bytes 7077896 | tf_op jit(solution)/shard_map/ppermute | solution.py:20
  5.5 40.7 %collective-permute-start.6 = (bf16[3072,384]{1,0:T(8,128)(2,1)S(1)}, bf16[3072,384]{1,0:T(8,128)(2,1)S(1)}, u32[]{:S(2)}, u32[]{:S(2)}) collective-permute-start(bf16[3072,384]{1,0:T(8,128)(2,1)S(1)} %shard_map.107), channel_id=1, source_target_pairs={{0,1},{1,0},{2,3},{3,2},{4,5},{5,4},{6,7},{7,6},{8,9},{9,8},{10,11... | collective-permute-start | bytes 7077896 | tf_op jit(solution)/shard_map/ppermute | solution.py:20
  17.9 10.2 %collective-permute-start.20 = (bf16[64,1536]{1,0:T(8,128)(2,1)S(1)}, bf16[64,1536]{1,0:T(8,128)(2,1)S(1)}, u32[]{:S(2)}, u32[]{:S(2)}) collective-permute-start(bf16[64,1536]{1,0:T(8,128)(2,1)S(1)} %get-tuple-element.59.refs_0_), channel_id=1, source_target_pairs={{0,4},{1,5},{2,6},{3,7},{4,0},{5,1},{6,2},{7,3},{8,12},{9,13},{10,... | collective-permute-start | bytes 589832 | tf_op jit(solution)/shard_map/ppermute | solution.py:20
  19.1 9.1 %collective-permute-start.21 = (bf16[64,1536]{1,0:T(8,128)(2,1)S(1)}, bf16[64,1536]{1,0:T(8,128)(2,1)S(1)}, u32[]{:S(2)}, u32[]{:S(2)}) collective-permute-start(bf16[64,1536]{1,0:T(8,128)(2,1)S(1)} %get-tuple-element.60.refs_2_), channel_id=1, source_target_pairs={{0,12},{1,13},{2,14},{3,15},{4,8},{5,9},{6,10},{7,11},{8,4},{9,5},... | collective-permute-start | bytes 589832 | tf_op jit(solution)/shard_map/ppermute | solution.py:20
  28.3 9.6 %collective-permute-start.22 = (bf16[128,1536]{1,0:T(8,128)(2,1)S(1)}, bf16[128,1536]{1,0:T(8,128)(2,1)S(1)}, u32[]{:S(2)}, u32[]{:S(2)}) collective-permute-start(bf16[128,1536]{1,0:T(8,128)(2,1)S(1)} %get-tuple-element.61.refs_0_), channel_id=1, source_target_pairs={{0,12},{1,13},{2,14},{3,15},{4,8},{5,9},{6,10},{7,11},{8,4},{9,5},... | collective-permute-start | bytes 1179656 | tf_op jit(solution)/shard_map/ppermute | solution.py:20
  35.9 10.4 %collective-permute-start.4 = (bf16[128,1536]{1,0:T(8,128)(2,1)S(1)}, bf16[128,1536]{1,0:T(8,128)(2,1)S(1)}, u32[]{:S(2)}, u32[]{:S(2)}) collective-permute-start(bf16[128,1536]{1,0:T(8,128)(2,1)S(1)} %get-tuple-element.43.refs_0_), channel_id=1, source_target_pairs={{0,12},{1,13},{2,14},{3,15},{4,8},{5,9},{6,10},{7,11},{8,4},{9,5},... | collective-permute-start | bytes 1179656 | tf_op jit(solution)/shard_map/ppermute | solution.py:20
  39.7 14.6 %collective-permute-start.24 = (f32[256,768]{1,0:T(8,128)S(1)}, f32[256,768]{1,0:T(8,128)S(1)}, u32[]{:S(2)}, u32[]{:S(2)}) collective-permute-start(f32[256,768]{1,0:T(8,128)S(1)} %shard_map.120.mine), channel_id=1, source_target_pairs={{0,1},{1,0},{2,3},{3,2},{4,5},{5,4},{6,7},{7,6},{8,9},{9,8},{10,11... | collective-permute-start | bytes 2359304 | tf_op jit(solution)/shard_map/ppermute | solution.py:20
  48.1 9.7 %collective-permute-start.7 = (f32[256,768]{1,0:T(8,128)S(1)}, f32[256,768]{1,0:T(8,128)S(1)}, u32[]{:S(2)}, u32[]{:S(2)}) collective-permute-start(f32[256,768]{1,0:T(8,128)S(1)} %shard_map.108.mine), channel_id=1, source_target_pairs={{0,1},{1,0},{2,3},{3,2},{4,5},{5,4},{6,7},{7,6},{8,9},{9,8},{10,11... | collective-permute-start | bytes 2359304 | tf_op jit(solution)/shard_map/ppermute | solution.py:20
  56.4 10.5 %collective-permute-start.25 = (bf16[128,1536]{1,0:T(8,128)(2,1)S(1)}, bf16[128,1536]{1,0:T(8,128)(2,1)S(1)}, u32[]{:S(2)}, u32[]{:S(2)}) collective-permute-start(bf16[128,1536]{1,0:T(8,128)(2,1)S(1)} %get-tuple-element.64), channel_id=1, source_target_pairs={{0,4},{1,5},{2,6},{3,7},{4,0},{5,1},{6,2},{7,3},{8,12},{9,13},{10,... | collective-permute-start | bytes 1179656 | tf_op jit(solution)/shard_map/ppermute | solution.py:20
  56.5 11.5 %collective-permute-start.26 = (bf16[128,1536]{1,0:T(8,128)(2,1)S(1)}, bf16[128,1536]{1,0:T(8,128)(2,1)S(1)}, u32[]{:S(2)}, u32[]{:S(2)}) collective-permute-start(bf16[128,1536]{1,0:T(8,128)(2,1)S(1)} %get-tuple-element.66), channel_id=1, source_target_pairs={{0,12},{1,13},{2,14},{3,15},{4,8},{5,9},{6,10},{7,11},{8,4},{9,5},... | collective-permute-start | bytes 1179656 | tf_op jit(solution)/shard_map/ppermute | solution.py:20
  59.9 15.4 %collective-permute-start.10 = (bf16[128,1536]{1,0:T(8,128)(2,1)S(1)}, bf16[128,1536]{1,0:T(8,128)(2,1)S(1)}, u32[]{:S(2)}, u32[]{:S(2)}) collective-permute-start(bf16[128,1536]{1,0:T(8,128)(2,1)S(1)} %get-tuple-element.46), channel_id=1, source_target_pairs={{0,4},{1,5},{2,6},{3,7},{4,0},{5,1},{6,2},{7,3},{8,12},{9,13},{10,... | collective-permute-start | bytes 1179656 | tf_op jit(solution)/shard_map/ppermute | solution.py:20
  60.8 15.7 %collective-permute-start.11 = (bf16[128,1536]{1,0:T(8,128)(2,1)S(1)}, bf16[128,1536]{1,0:T(8,128)(2,1)S(1)}, u32[]{:S(2)}, u32[]{:S(2)}) collective-permute-start(bf16[128,1536]{1,0:T(8,128)(2,1)S(1)} %get-tuple-element.48), channel_id=1, source_target_pairs={{0,12},{1,13},{2,14},{3,15},{4,8},{5,9},{6,10},{7,11},{8,4},{9,5},... | collective-permute-start | bytes 1179656 | tf_op jit(solution)/shard_map/ppermute | solution.py:20
  68.2 9.7 %collective-permute-start.27 = (bf16[64,3072]{1,0:T(8,128)(2,1)S(1)}, bf16[64,3072]{1,0:T(8,128)(2,1)S(1)}, u32[]{:S(2)}, u32[]{:S(2)}) collective-permute-start(bf16[64,3072]{1,0:T(8,128)(2,1)S(1)} %get-tuple-element.68), channel_id=1, source_target_pairs={{0,2},{1,3},{2,0},{3,1},{4,6},{5,7},{6,4},{7,5},{8,10},{9,11},{10,... | collective-permute-start | bytes 1179656 | tf_op jit(solution)/shard_map/ppermute | solution.py:20
  76.6 12.6 %collective-permute-start.12 = (bf16[64,1536]{1,0:T(8,128)(2,1)S(1)}, bf16[64,1536]{1,0:T(8,128)(2,1)S(1)}, u32[]{:S(2)}, u32[]{:S(2)}) collective-permute-start(bf16[64,1536]{1,0:T(8,128)(2,1)S(1)} %get-tuple-element.50), channel_id=1, source_target_pairs={{0,12},{1,13},{2,14},{3,15},{4,8},{5,9},{6,10},{7,11},{8,4},{9,5},... | collective-permute-start | bytes 589832 | tf_op jit(solution)/shard_map/ppermute | solution.py:20
  77.9 11.3 %collective-permute-start.13 = (bf16[64,1536]{1,0:T(8,128)(2,1)S(1)}, bf16[64,1536]{1,0:T(8,128)(2,1)S(1)}, u32[]{:S(2)}, u32[]{:S(2)}) collective-permute-start(bf16[64,1536]{1,0:T(8,128)(2,1)S(1)} %get-tuple-element.52), channel_id=1, source_target_pairs={{0,4},{1,5},{2,6},{3,7},{4,0},{5,1},{6,2},{7,3},{8,12},{9,13},{10,... | collective-permute-start | bytes 589832 | tf_op jit(solution)/shard_map/ppermute | solution.py:20
  78.0 14.1 %collective-permute-start.28 = (bf16[32,1536]{1,0:T(8,128)(2,1)S(1)}, bf16[32,1536]{1,0:T(8,128)(2,1)S(1)}, u32[]{:S(2)}, u32[]{:S(2)}) collective-permute-start(bf16[32,1536]{1,0:T(8,128)(2,1)S(1)} %get-tuple-element.70), channel_id=1, source_target_pairs={{0,12},{1,13},{2,14},{3,15},{4,8},{5,9},{6,10},{7,11},{8,4},{9,5},... | collective-permute-start | bytes 294920 | tf_op jit(solution)/shard_map/ppermute | solution.py:20
  79.5 12.5 %collective-permute-start.29 = (bf16[32,1536]{1,0:T(8,128)(2,1)S(1)}, bf16[32,1536]{1,0:T(8,128)(2,1)S(1)}, u32[]{:S(2)}, u32[]{:S(2)}) collective-permute-start(bf16[32,1536]{1,0:T(8,128)(2,1)S(1)} %get-tuple-element.72), channel_id=1, source_target_pairs={{0,4},{1,5},{2,6},{3,7},{4,0},{5,1},{6,2},{7,3},{8,12},{9,13},{10,... | collective-permute-start | bytes 294920 | tf_op jit(solution)/shard_map/ppermute | solution.py:20
  81.0 23.4 %collective-permute-start.31 = (bf16[16,6144]{1,0:T(8,128)(2,1)S(1)}, bf16[16,6144]{1,0:T(8,128)(2,1)S(1)}, u32[]{:S(2)}, u32[]{:S(2)}) collective-permute-start(bf16[16,6144]{1,0:T(8,128)(2,1)S(1)} %shard_map.125), channel_id=1, source_target_pairs={{0,240},{16,224},{32,208},{48,192},{64,176},{80,160},{96,144},{112... | collective-permute-start | bytes 589832 | tf_op jit(solution)/shard_map/ppermute | solution.py:338
  89.3 12.3 %collective-permute-start.15 = (f32[16,3072]{1,0:T(8,128)S(1)}, f32[16,3072]{1,0:T(8,128)S(1)}, u32[]{:S(2)}, u32[]{:S(2)}) collective-permute-start(f32[16,3072]{1,0:T(8,128)S(1)} %get-tuple-element.55), channel_id=1, source_target_pairs={{0,1},{1,0},{2,3},{3,2},{4,5},{5,4},{6,7},{7,6},{8,9},{9,8},{10,11... | collective-permute-start | bytes 589832 | tf_op jit(solution)/shard_map/ppermute | solution.py:20
  92.1 12.3 %collective-permute-start.30 = (f32[16,3072]{1,0:T(8,128)S(1)}, f32[16,3072]{1,0:T(8,128)S(1)}, u32[]{:S(2)}, u32[]{:S(2)}) collective-permute-start(f32[16,3072]{1,0:T(8,128)S(1)} %get-tuple-element.74), channel_id=1, source_target_pairs={{0,1},{1,0},{2,3},{3,2},{4,5},{5,4},{6,7},{7,6},{8,9},{9,8},{10,11... | collective-permute-start | bytes 589832 | tf_op jit(solution)/shard_map/ppermute | solution.py:20
  93.1 8.6 %collective-permute-start.16 = (bf16[16,3072]{1,0:T(8,128)(2,1)S(1)}, bf16[16,3072]{1,0:T(8,128)(2,1)S(1)}, u32[]{:S(2)}, u32[]{:S(2)}) collective-permute-start(bf16[16,3072]{1,0:T(8,128)(2,1)S(1)} %get-tuple-element.56), channel_id=1, source_target_pairs={{0,3},{1,2},{2,1},{3,0},{4,7},{5,6},{6,5},{7,4},{8,11},{9,10},{10,... | collective-permute-start | bytes 294920 | tf_op jit(solution)/shard_map/ppermute | solution.py:20
  99.0 14.5 %collective-permute-start.33 = (bf16[16,6144]{1,0:T(8,128)(2,1)S(1)}, bf16[16,6144]{1,0:T(8,128)(2,1)S(1)}, u32[]{:S(2)}, u32[]{:S(2)}) collective-permute-start(bf16[16,6144]{1,0:T(8,128)(2,1)S(1)} %bitcast.24), channel_id=1, source_target_pairs={{0,240},{16,224},{32,208},{48,192},{64,176},{80,160},{96,144},{112... | collective-permute-start | bytes 589832 | tf_op jit(solution)/shard_map/ppermute | solution.py:337
  101.7 20.0 %collective-permute-start.17 = (bf16[16,6144]{1,0:T(8,128)(2,1)S(1)}, bf16[16,6144]{1,0:T(8,128)(2,1)S(1)}, u32[]{:S(2)}, u32[]{:S(2)}) collective-permute-start(bf16[16,6144]{1,0:T(8,128)(2,1)S(1)} %shard_map.114), channel_id=1, source_target_pairs={{0,16},{16,32},{32,48},{48,64},{64,80},{80,96},{96,112},{112,128},... | collective-permute-start | bytes 589832 | tf_op jit(solution)/shard_map/ppermute | solution.py:377
  104.7 17.7 %collective-permute-start.32 = (bf16[16,6144]{1,0:T(8,128)(2,1)S(1)}, bf16[16,6144]{1,0:T(8,128)(2,1)S(1)}, u32[]{:S(2)}, u32[]{:S(2)}) collective-permute-start(bf16[16,6144]{1,0:T(8,128)(2,1)S(1)} %shard_map.126), channel_id=1, source_target_pairs={{0,240},{16,0},{32,16},{48,32},{64,48},{80,64},{96,80},{112,96},{1... | collective-permute-start | bytes 589832 | tf_op jit(solution)/shard_map/ppermute | solution.py:376
  (20 other events, 183.3 us)
